TPU v7x, 256 devices: a whole 4x4x8 slice. The times are simulated.
256 devices in a mesh: patch: 32 (over y, x, core), rhs: 8 (over z).
Axes of the slice: x: 4, y: 4, z: 8, core: 2. Of those that a mesh axis runs over, the one named last changes fastest.
Arguments:
- rhs_vectors: float32 [256, 16, 384], P('patch', 'rhs'), may hold values from -8 to 8
- near_blocks: bfloat16 [256, 4, 384, 384], P('patch'), may hold values from -1 to 5, as said below
- neighbours: int32 [256, 4], P('patch'), may hold values from 0 to 255, as said below
- up_maps: float32 [256, 64, 384], P('patch'), may hold values from -0.3125 to 0.3125
- shift_up: float32 [256, 64, 64], P('patch'), may hold values from -0.25 to 0.25
- far_lists: int32 [32, 4], P('patch'), may hold values from 0 to 31, as said below
- translations: float32 [32, 4, 64, 64], P('patch'), may hold values from -0.375 to 0.375
- shift_down: float32 [256, 64, 64], P('patch'), may hold values from -0.75 to 0.75
- down_maps: float32 [256, 384, 64], P('patch'), may hold values from -0.375 to 0.375
Outputs:
- solution: float32 [256, 16, 384], P('patch', 'rhs')
- residual: float32 [256, 16, 384], P('patch', 'rhs')
Inputs may be any that keep to these rules, and one draw needn't show every extreme that they name: `neighbours`: entry 0 of each row is the patch itself; every other entry names a patch of the same cell or of the cell just before or just after it, cyclically. `far_lists`: entry 0 of each row names the cell just before or just after the row's own cell, cyclically, and for cell 0 the cell just before it; every other entry names a cell other than the row's own. `near_blocks`: the blocks keep the operator's symmetric part positive definite.
All inputs are finite; a program needn't handle non-finite values.
Results may differ from a plain program's by a relative error of at most 0.008.
The roundings to bfloat16 on the way count: a program that leaves them out, or rounds other values in their place, can miss the bound.
Values may be sent and summed in bfloat16 or wider, within the bound.
A program may use at most 64 MiB of HBM per device.

v0:
```python
import jax
import jax.numpy as jnp
from jax import lax
from jax.sharding import PartitionSpec as P

ITERS = 2


HIGH = lax.Precision.HIGHEST


def from_everyone(array, axis):
    devices = lax.axis_size(axis)
    return lax.all_to_all(
        jnp.broadcast_to(array[None], (devices, *array.shape)), axis, 0, 0, tiled=True
    )


def taken_together(array, axis):
    return from_everyone(array, axis).sum(axis=0)


def with_halo(block, sides, width):
    for axis, dim in sides:
        count = lax.axis_size(axis)
        forward = [(i, i + 1) for i in range(count - 1)]
        forward.append((count - 1, 0))
        backward = [(target, source) for source, target in forward]
        low = lax.ppermute(
            lax.slice_in_dim(block, block.shape[dim] - width, None, axis=dim), axis, forward
        )
        high = lax.ppermute(lax.slice_in_dim(block, 0, width, axis=dim), axis, backward)
        block = jnp.concatenate([low, block, high], axis=dim)
    return block


def laid_out(parts, dim):
    parts = jnp.moveaxis(parts, 0, dim)
    lengths = parts.shape
    return parts.reshape(*lengths[:dim], lengths[dim] * lengths[dim + 1], *lengths[dim + 2 :])


def collect(array, axis, dim):
    parts = from_everyone(array, axis)
    return laid_out(parts, dim)


def spd_solve(matrix, right):
    factor = jnp.linalg.cholesky(matrix)
    return jax.scipy.linalg.cho_solve((factor, True), right)


def gram(left, right):
    return jnp.einsum("pkw,plw->kl", left, right, precision=HIGH)


def mix(field, coeffs):
    return jnp.einsum("pkw,kl->plw", field, coeffs, precision=HIGH)


def residual_sum(residual):
    return taken_together(gram(residual, residual), "patch")


def apply_operator(
    field,
    near_blocks,
    neighbours,
    up_maps,
    shift_up,
    far_lists,
    translations,
    shift_down,
    down_maps,
):
    patches = field.shape[0]
    count = lax.axis_size("patch")
    first = lax.axis_index("patch") * patches - patches
    rounded = field.astype(jnp.bfloat16)
    widened = with_halo(rounded, (("patch", 0),), patches)
    local_ids = jnp.mod(neighbours - first, patches * count)
    picked = widened[local_ids]
    near = jnp.einsum("pjvw,pjkw->pkv", near_blocks, picked, preferred_element_type=jnp.float32)
    moments = jnp.einsum("pew,pkw->pke", up_maps, field, precision=HIGH)
    cell_moment = jnp.einsum("pfe,pke->kf", shift_up, moments, precision=HIGH)
    sources = far_lists[0]
    table = translations[0]
    piece = collect(cell_moment[None], "patch", 0)
    labels = jnp.arange(piece.shape[0], dtype=jnp.int32)
    select = (sources[:, None] == labels[None, :]).astype(jnp.float32)
    chosen = jnp.einsum("ji,ike->jke", select, piece, precision=HIGH)
    local_exp = jnp.zeros_like(cell_moment) + jnp.einsum(
        "jfe,jke->kf", table, chosen, precision=HIGH
    )
    patch_exp = jnp.einsum("pfe,ke->pkf", shift_down, local_exp, precision=HIGH)
    far = jnp.einsum("pvf,pkf->pkv", down_maps, patch_exp, precision=HIGH)
    return near + far


def on_device(
    rhs_vectors,
    near_blocks,
    neighbours,
    up_maps,
    shift_up,
    far_lists,
    translations,
    shift_down,
    down_maps,
):
    my_cols = rhs_vectors.shape[1]
    offset = lax.axis_index("rhs") * my_cols
    residual = collect(rhs_vectors, "rhs", 1)
    solution = jnp.zeros_like(residual)
    direction = residual
    current = jnp.zeros((residual.shape[1], residual.shape[1]), jnp.float32)
    for step in range(ITERS):
        image = apply_operator(
            direction,
            near_blocks,
            neighbours,
            up_maps,
            shift_up,
            far_lists,
            translations,
            shift_down,
            down_maps,
        )
        if step == 0:
            current = residual_sum(residual)
        curve = taken_together(gram(direction, image), "patch")
        curve = 0.5 * (curve + curve.T)
        alpha = spd_solve(curve, current)
        solution = solution + mix(direction, alpha)
        residual = residual - mix(image, alpha)
        if step + 1 < ITERS:
            following = residual_sum(residual)
            beta = spd_solve(current, following)
            direction = residual + mix(direction, beta)
            current = following
    solution_mine = lax.dynamic_slice_in_dim(solution, offset, my_cols, 1)
    residual_mine = lax.dynamic_slice_in_dim(residual, offset, my_cols, 1)
    return (solution_mine, residual_mine)


def solution(mesh):
    return jax.shard_map(
        on_device,
        mesh=mesh,
        in_specs=(
            P("patch", "rhs", None),
            P("patch", None, None, None),
            P("patch", None),
            P("patch", None, None),
            P("patch", None, None),
            P("patch", None),
            P("patch", None, None, None),
            P("patch", None, None),
            P("patch", None, None),
        ),
        out_specs=(P("patch", "rhs", None), P("patch", "rhs", None)),
        check_vma=False,
    )
```

profile of v0, /device:TPU:1, one launch (start us, length us, event | category | flops | bytes accessed | tf_op | source)
XLA Modules:
  0.0 139.1 jit_solution(15504959503871310235)
XLA Ops:
  0.6 1.5 %broadcast_in_dim.16 = f32[8,8,2,384]{3,2,1,0:T(2,128)} broadcast(f32[8,2,384]{2,1,0:T(2,128)} %param.12), dimensions={1,2,3} | broadcast | bytes 221184 | tf_op jit(solution)/shard_map/broadcast_in_dim | solution.py:15
  2.2 9.0 %all-to-all-start = ((f32[8,8,2,384]{3,2,1,0:T(2,128)}), f32[8,8,2,384]{3,2,1,0:T(2,128)S(1)}, u32[]{:S(2)}, u32[]{:S(2)}) async-start(f32[8,8,2,384]{3,2,1,0:T(2,128)} %broadcast_in_dim.16), calls=%async_computation | async-start | bytes 393216 | tf_op jit(solution)/shard_map/all_to_all | solution.py:14
  11.2 0.7 compare_select_fusion
  12.0 8.1 %all-to-all-done = f32[8,8,2,384]{3,2,1,0:T(2,128)S(1)} async-done(((f32[8,8,2,384]{3,2,1,0:T(2,128)}), f32[8,8,2,384]{3,2,1,0:T(2,128)S(1)}, u32[]{:S(2)}, u32[]{:S(2)}) %all-to-all-start) | async-done | bytes 196640 | tf_op jit(solution)/shard_map/all_to_all | solution.py:14
  20.4 0.3 convolution_bitcast_fusion.14
  20.8 2.5 %collective-permute-start.1 = (bf16[8,16,384]{2,1,0:T(8,128)(2,1)S(1)}, bf16[8,16,384]{2,1,0:T(8,128)(2,1)S(1)}, u32[]{:S(2)}, u32[]{:S(2)}) collective-permute-start(bf16[8,16,384]{2,1,0:T(8,128)(2,1)S(1)} %convert_element_type.8), channel_id=1, source_target_pairs={{8,0},{16,8},{24,16},{32,24},{40,32},{48,40},{56,48},{64,56},{72,6... | collective-permute-start | bytes 294920 | tf_op jit(solution)/shard_map/ppermute | solution.py:32
  23.3 1.2 collective-permute-start
  24.5 2.1 %fusion.39 = f32[8,16,64]{2,1,0:T(8,128)S(1)} fusion(f32[8,16,384]{2,1,0:T(8,128)S(1)} %reshape.35, f32[8,64,384]{2,1,0:T(8,128)} %param.15), kind=kOutput, calls=%fused_computation.83 | convolution fusion | flops 37748736 | bytes 1015808 | tf_op jit(solution)/shard_map/pew,pkw->pke/dot_general | solution.py:84
  26.6 0.7 reshape.76
  27.3 8.2 %all-to-all-start.3 = ((f32[32,1,256]{2,1,0:T(1,128)}), f32[32,1,256]{2,1,0:T(1,128)S(1)}, u32[]{:S(2)}, u32[]{:S(2)}) async-start(f32[32,1,256]{2,1,0:T(1,128)} %reshape.76), calls=%async_computation.3 | async-start | bytes 65536 | tf_op jit(solution)/shard_map/all_to_all | solution.py:14
  35.5 1.2 convolution_bitcast_fusion.11
  36.8 0.8 reshape.78
  37.6 5.1 %all-to-all-done.3 = f32[32,1,256]{2,1,0:T(1,128)S(1)} async-done(((f32[32,1,256]{2,1,0:T(1,128)}), f32[32,1,256]{2,1,0:T(1,128)S(1)}, u32[]{:S(2)}, u32[]{:S(2)}) %all-to-all-start.3) | async-done | bytes 32800 | tf_op jit(solution)/shard_map/all_to_all | solution.py:14
  42.8 3.9 %all-to-all-start.1 = ((f32[32,1,1024]{2,1,0:T(1,128)}), f32[32,1,1024]{2,1,0:T(1,128)S(1)}, u32[]{:S(2)}, u32[]{:S(2)}) async-start(f32[32,1,1024]{2,1,0:T(1,128)} %reshape.78), calls=%async_computation.1 | async-start | bytes 262144 | tf_op jit(solution)/shard_map/all_to_all | solution.py:14
  46.7 0.5 broadcast.84
  47.2 0.7 reduce.4
  48.2 1.5 %cholesky.70 = f32[16,16]{1,0:T(8,128)S(1)} custom-call(f32[16,16]{1,0:T(8,128)S(1)} %fusion.26), custom_call_target="Cholesky" | custom-call | tf_op jit(solution)/shard_map/jit(cholesky)/cholesky | solution.py:49
  49.7 0.6 gather_fusion
  50.4 6.3 %convolution_bitcast_fusion.4 = f32[8,16,384]{2,1,0:T(8,128)S(1)} fusion(bf16[8,4,16,384]{3,2,1,0:T(8,128)(2,1)S(1)} %bitcast.151, bf16[8,4,384,384]{3,2,1,0:T(8,128)(2,1)} %param.13), kind=kOutput, calls=%fused_computation.10 | convolution fusion | flops 150994944 | bytes 10027008 | tf_op jit(solution)/shard_map/pjvw,pjkw->pkv/dot_general | solution.py:83
  56.7 1.0 reduce.5
  58.3 0.7 convolution_bitcast_fusion.6
  59.0 0.6 convolution_add_fusion.1
  59.7 0.3 convolution_bitcast_fusion.15
  60.2 0.8 reshape.80
  60.9 7.5 %all-to-all-start.2 = ((f32[32,1,256]{2,1,0:T(1,128)}), f32[32,1,256]{2,1,0:T(1,128)S(1)}, u32[]{:S(2)}, u32[]{:S(2)}) async-start(f32[32,1,256]{2,1,0:T(1,128)} %reshape.80), calls=%async_computation.2 | async-start | bytes 65536 | tf_op jit(solution)/shard_map/all_to_all | solution.py:14
  68.4 0.7 compare_reduce_fusion.1
  69.1 6.6 %all-to-all-done.2 = f32[32,1,256]{2,1,0:T(1,128)S(1)} async-done(((f32[32,1,256]{2,1,0:T(1,128)}), f32[32,1,256]{2,1,0:T(1,128)S(1)}, u32[]{:S(2)}, u32[]{:S(2)}) %all-to-all-start.2) | async-done | bytes 32800 | tf_op jit(solution)/shard_map/all_to_all | solution.py:14
  75.7 0.7 reduce.6
  76.7 1.5 %cholesky.59 = f32[16,16]{1,0:T(8,128)S(1)} custom-call(f32[16,16]{1,0:T(8,128)S(1)} %fusion.30), custom_call_target="Cholesky" | custom-call | tf_op jit(solution)/shard_map/jit(cholesky)/cholesky | solution.py:49
  78.2 0.6 compare_reduce_fusion.2
  78.9 0.6 fusion.15
  79.5 1.2 custom-call.9
  81.1 0.3 fusion.1
  81.5 0.3 convolution_bitcast_fusion.13
  81.9 0.8 reshape.82
  82.6 3.9 %all-to-all-start.4 = ((f32[32,1,256]{2,1,0:T(1,128)}), f32[32,1,256]{2,1,0:T(1,128)S(1)}, u32[]{:S(2)}, u32[]{:S(2)}) async-start(f32[32,1,256]{2,1,0:T(1,128)} %reshape.82), calls=%async_computation.4 | async-start | bytes 65536 | tf_op jit(solution)/shard_map/all_to_all | solution.py:14
  86.5 0.6 fusion.16
  87.2 1.2 custom-call.10
  88.4 5.5 %all-to-all-done.4 = f32[32,1,256]{2,1,0:T(1,128)S(1)} async-done(((f32[32,1,256]{2,1,0:T(1,128)}), f32[32,1,256]{2,1,0:T(1,128)S(1)}, u32[]{:S(2)}, u32[]{:S(2)}) %all-to-all-start.4) | async-done | bytes 32800 | tf_op jit(solution)/shard_map/all_to_all | solution.py:14
  93.9 0.7 reduce.7
  95.2 0.3 fusion.38
  95.5 0.5 collective-permute-start.3
  96.0 1.4 collective-permute-start.2
  97.3 0.9 fusion.41
  98.6 0.8 reshape.84
  99.5 6.6 %all-to-all-start.5 = ((f32[32,1,1024]{2,1,0:T(1,128)}), f32[32,1,1024]{2,1,0:T(1,128)S(1)}, u32[]{:S(2)}, u32[]{:S(2)}) async-start(f32[32,1,1024]{2,1,0:T(1,128)} %reshape.84), calls=%async_computation.5 | async-start | bytes 262144 | tf_op jit(solution)/shard_map/all_to_all | solution.py:14
  106.1 0.6 gather_fusion.1
  106.8 6.2 %convolution_bitcast_fusion.3 = f32[8,16,384]{2,1,0:T(8,128)S(1)} fusion(bf16[8,4,16,384]{3,2,1,0:T(8,128)(2,1)S(1)} %bitcast.150, bf16[8,4,384,384]{3,2,1,0:T(8,128)(2,1)} %param.13), kind=kOutput, calls=%fused_computation.9 | convolution fusion | flops 150994944 | bytes 10027008 | tf_op jit(solution)/shard_map/pjvw,pjkw->pkv/dot_general | solution.py:83
  113.0 0.7 all-to-all-done.5
  113.7 1.0 reduce.8
  115.2 0.7 convolution_bitcast_fusion.5
  115.9 0.6 convolution_add_fusion
  116.5 0.3 convolution_bitcast_fusion.12
  117.0 0.8 reshape.86
  117.7 6.7 %all-to-all-start.6 = ((f32[32,1,256]{2,1,0:T(1,128)}), f32[32,1,256]{2,1,0:T(1,128)S(1)}, u32[]{:S(2)}, u32[]{:S(2)}) async-start(f32[32,1,256]{2,1,0:T(1,128)} %reshape.86), calls=%async_computation.6 | async-start | bytes 65536 | tf_op jit(solution)/shard_map/all_to_all | solution.py:14
  124.8 6.9 %all-to-all-done.6 = f32[32,1,256]{2,1,0:T(1,128)S(1)} async-done(((f32[32,1,256]{2,1,0:T(1,128)}), f32[32,1,256]{2,1,0:T(1,128)S(1)}, u32[]{:S(2)}, u32[]{:S(2)}) %all-to-all-start.6) | async-done | bytes 32800 | tf_op jit(solution)/shard_map/all_to_all | solution.py:14
  131.7 0.7 reduce.9
  132.8 1.5 %cholesky.81 = f32[16,16]{1,0:T(8,128)S(1)} custom-call(f32[16,16]{1,0:T(8,128)S(1)} %fusion.21), custom_call_target="Cholesky" | custom-call | tf_op jit(solution)/shard_map/jit(cholesky)/cholesky | solution.py:49
  134.3 0.6 compare_reduce_fusion
  134.9 0.6 fusion.17
  135.6 1.2 custom-call.11
  137.2 0.3 convolution_bitcast_fusion
  137.8 0.6 dynamic-slice_subtract_fusion
  138.5 0.6 fusion.14
  (68 shorter events, 5.3 us)
Async XLA Ops:
  0.6 58.4 %copy-start = (f32[8,384,64]{1,2,0:T(8,128)S(1)}, f32[8,384,64]{1,2,0:T(8,128)}, u32[]{:S(2)}) copy-start(f32[8,384,64]{1,2,0:T(8,128)} %param.20) | copy-start | bytes 2359300
  2.2 18.0 %all-to-all-start = ((f32[8,8,2,384]{3,2,1,0:T(2,128)}), f32[8,8,2,384]{3,2,1,0:T(2,128)S(1)}, u32[]{:S(2)}, u32[]{:S(2)}) async-start(f32[8,8,2,384]{3,2,1,0:T(2,128)} %broadcast_in_dim.16), calls=%async_computation | async-start | bytes 393216 | tf_op jit(solution)/shard_map/all_to_all | solution.py:14
  20.8 28.9 %collective-permute-start.1 = (bf16[8,16,384]{2,1,0:T(8,128)(2,1)S(1)}, bf16[8,16,384]{2,1,0:T(8,128)(2,1)S(1)}, u32[]{:S(2)}, u32[]{:S(2)}) collective-permute-start(bf16[8,16,384]{2,1,0:T(8,128)(2,1)S(1)} %convert_element_type.8), channel_id=1, source_target_pairs={{8,0},{16,8},{24,16},{32,24},{40,32},{48,40},{56,48},{64,56},{72,6... | collective-permute-start | bytes 294920 | tf_op jit(solution)/shard_map/ppermute | solution.py:32
  23.3 26.4 %collective-permute-start = (bf16[8,16,384]{2,1,0:T(8,128)(2,1)S(1)}, bf16[8,16,384]{2,1,0:T(8,128)(2,1)S(1)}, u32[]{:S(2)}, u32[]{:S(2)}) collective-permute-start(bf16[8,16,384]{2,1,0:T(8,128)(2,1)S(1)} %convert_element_type.8), channel_id=1, source_target_pairs={{0,8},{8,16},{16,24},{24,32},{32,40},{40,48},{48,56},{56,64},{64,7... | collective-permute-start | bytes 294920 | tf_op jit(solution)/shard_map/ppermute | solution.py:29
  27.3 15.5 %all-to-all-start.3 = ((f32[32,1,256]{2,1,0:T(1,128)}), f32[32,1,256]{2,1,0:T(1,128)S(1)}, u32[]{:S(2)}, u32[]{:S(2)}) async-start(f32[32,1,256]{2,1,0:T(1,128)} %reshape.76), calls=%async_computation.3 | async-start | bytes 65536 | tf_op jit(solution)/shard_map/all_to_all | solution.py:14
  42.8 14.0 %all-to-all-start.1 = ((f32[32,1,1024]{2,1,0:T(1,128)}), f32[32,1,1024]{2,1,0:T(1,128)S(1)}, u32[]{:S(2)}, u32[]{:S(2)}) async-start(f32[32,1,1024]{2,1,0:T(1,128)} %reshape.78), calls=%async_computation.1 | async-start | bytes 262144 | tf_op jit(solution)/shard_map/all_to_all | solution.py:14
  49.7 8.1 %copy-start.5 = (s32[1,4]{1,0:T(1,128)S(1)}, s32[1,4]{1,0:T(1,128)}, u32[]{:S(2)}) copy-start(s32[1,4]{1,0:T(1,128)} %param.17) | copy-start | bytes 52
  49.7 8.4 %copy-start.4 = (f32[1,4,64,64]{3,2,1,0:T(8,128)S(1)}, f32[1,4,64,64]{3,2,1,0:T(8,128)}, u32[]{:S(2)}) copy-start(f32[1,4,64,64]{3,2,1,0:T(8,128)} %param.18) | copy-start | bytes 196612
  50.4 7.9 %copy-start.3 = (f32[8,64,64]{2,1,0:T(8,128)S(1)}, f32[8,64,64]{2,1,0:T(8,128)}, u32[]{:S(2)}) copy-start(f32[8,64,64]{2,1,0:T(8,128)} %param.19) | copy-start | bytes 393220
  50.4 47.0 %copy-start.1 = (f32[8,64,384]{2,1,0:T(8,128)S(1)}, f32[8,64,384]{2,1,0:T(8,128)}, u32[]{:S(2)}) copy-start(f32[8,64,384]{2,1,0:T(8,128)} %param.15) | copy-start | bytes 2359300
  50.4 47.9 %copy-start.2 = (f32[8,64,64]{2,1,0:T(8,128)S(1)}, f32[8,64,64]{2,1,0:T(8,128)}, u32[]{:S(2)}) copy-start(f32[8,64,64]{2,1,0:T(8,128)} %param.16) | copy-start | bytes 393220
  60.9 14.8 %all-to-all-start.2 = ((f32[32,1,256]{2,1,0:T(1,128)}), f32[32,1,256]{2,1,0:T(1,128)S(1)}, u32[]{:S(2)}, u32[]{:S(2)}) async-start(f32[32,1,256]{2,1,0:T(1,128)} %reshape.80), calls=%async_computation.2 | async-start | bytes 65536 | tf_op jit(solution)/shard_map/all_to_all | solution.py:14
  82.6 11.3 %all-to-all-start.4 = ((f32[32,1,256]{2,1,0:T(1,128)}), f32[32,1,256]{2,1,0:T(1,128)S(1)}, u32[]{:S(2)}, u32[]{:S(2)}) async-start(f32[32,1,256]{2,1,0:T(1,128)} %reshape.82), calls=%async_computation.4 | async-start | bytes 65536 | tf_op jit(solution)/shard_map/all_to_all | solution.py:14
  95.5 10.5 %collective-permute-start.3 = (bf16[8,16,384]{2,1,0:T(8,128)(2,1)S(1)}, bf16[8,16,384]{2,1,0:T(8,128)(2,1)S(1)}, u32[]{:S(2)}, u32[]{:S(2)}) collective-permute-start(bf16[8,16,384]{2,1,0:T(8,128)(2,1)S(1)} %get-tuple-element.4), channel_id=1, source_target_pairs={{8,0},{16,8},{24,16},{32,24},{40,32},{48,40},{56,48},{64,56},{72,6... | collective-permute-start | bytes 294920 | tf_op jit(solution)/shard_map/ppermute | solution.py:32
  96.0 10.1 %collective-permute-start.2 = (bf16[8,16,384]{2,1,0:T(8,128)(2,1)S(1)}, bf16[8,16,384]{2,1,0:T(8,128)(2,1)S(1)}, u32[]{:S(2)}, u32[]{:S(2)}) collective-permute-start(bf16[8,16,384]{2,1,0:T(8,128)(2,1)S(1)} %get-tuple-element.4), channel_id=1, source_target_pairs={{0,8},{8,16},{16,24},{24,32},{32,40},{40,48},{48,56},{56,64},{64,7... | collective-permute-start | bytes 294920 | tf_op jit(solution)/shard_map/ppermute | solution.py:29
  99.5 14.2 %all-to-all-start.5 = ((f32[32,1,1024]{2,1,0:T(1,128)}), f32[32,1,1024]{2,1,0:T(1,128)S(1)}, u32[]{:S(2)}, u32[]{:S(2)}) async-start(f32[32,1,1024]{2,1,0:T(1,128)} %reshape.84), calls=%async_computation.5 | async-start | bytes 262144 | tf_op jit(solution)/shard_map/all_to_all | solution.py:14
  117.7 14.0 %all-to-all-start.6 = ((f32[32,1,256]{2,1,0:T(1,128)}), f32[32,1,256]{2,1,0:T(1,128)S(1)}, u32[]{:S(2)}, u32[]{:S(2)}) async-start(f32[32,1,256]{2,1,0:T(1,128)} %reshape.86), calls=%async_computation.6 | async-start | bytes 65536 | tf_op jit(solution)/shard_map/all_to_all | solution.py:14
where the time goes:
time: 140 us; the launch traced here: 139 us
  starting transfers between devices  51.4 us (37%)
  waiting for transfers between devices  33 us (24%)
  matrix products  24.7 us (18%)
  other arithmetic  19.1 us (14%)
  local copies, waits for them, and re-layouts  9.85 us (7%)
    all_to_all x7, starting transfers between devices, from_everyone(): lax.all_to_all(jnp.broadcast_to(array[None], (devices, *array.shape)), ax...  45.8 us
    all_to_all x7, waiting for transfers between devices, from_everyone(): lax.all_to_all(jnp.broadcast_to(array[None], (devices, *array.shape)), ax...  33 us
    dot_general x2, matrix products, apply_operator(): jnp.einsum('pjvw,pjkw->pkv', near_blocks, picked, preferred_element_type=...  12.5 us
    another operation x9, other arithmetic, spd_solve(): factor = jnp.linalg.cholesky(matrix)  6.4 us
    another operation x6, other arithmetic, spd_solve(): return jax.scipy.linalg.cho_solve((factor, True), right)  5.62 us
    unnamed x24, local copies, waits for them, and re-layouts  5.38 us
    all_to_all x6, other arithmetic, from_everyone(): lax.all_to_all(jnp.broadcast_to(array[None], (devices, *array.shape)), ax...  4.8 us
    dot_general x2, matrix products, apply_operator(): moments = jnp.einsum('pew,pkw->pke', up_maps, field, precision=HIGH)  2.98 us
  transfers between devices with their start and end apart: 11, of which 6 were waited for; matrix products, arithmetic and copies ran while one was open for 20% of the time, Pallas kernels for 0%

commit v1 on v0

v1 whole, which is shorter than its diff:
```python
import jax
import jax.numpy as jnp
from jax import lax
from jax.experimental import pallas as pl
from jax.experimental.pallas import tpu as pltpu
from jax.sharding import PartitionSpec as P

F32 = jnp.float32
BF16 = jnp.bfloat16
HIGH = lax.Precision.HIGHEST
MESH = pl.DeviceIdType.MESH
PD, K, W, E, NB, FL = 8, 16, 384, 64, 4, 4
NT = (((1,), (1,)), ((), ()))
NN = (((1,), (0,)), ((), ()))


def dot(a, b, dims=NT, precision=None):
    return lax.dot_general(a, b, dims, precision=precision, preferred_element_type=F32)


def split(x):
    hi = x.astype(BF16)
    return hi, (x - hi.astype(F32)).astype(BF16)


def folded(x):
    return x + pltpu.roll(x, 64, 1)


def lane_of(shape):
    return lax.broadcasted_iota(jnp.int32, shape, 1)


def eliminate(top, *others):
    a = jnp.concatenate((top, *others), axis=0)
    lanes = lane_of(a.shape)
    for k in range(K):
        column = a[:, k : k + 1]
        row = a[k : k + 1, :]
        inverse = 1.0 / a[k : k + 1, k : k + 1]
        a = jnp.where(lanes == k, column * inverse, a - column * (row * inverse))
    return [a[K * (i + 1) : K * (i + 2), :] for i in range(len(others))]


def packed_grams(stack):
    full = dot(stack, stack)
    full = jnp.concatenate((full, jnp.zeros((4 * K, 128 - 4 * K), F32)), axis=1)

    def half(top, low):
        t = top + low
        t = t + pltpu.roll(t, 128 - K, 1)
        even = (lane_of((8, 128)) // K) % 2 == 0
        return jnp.where(even, t[:8], pltpu.roll(t[8:], K, 1))

    a = half(full[:K], full[K : 2 * K])
    b = half(full[2 * K : 3 * K], full[3 * K :])
    return jnp.where(lane_of((8, 128)) < 4 * K, a, pltpu.roll(b, 4 * K, 1))


def unpacked_grams(total):
    t = jnp.concatenate((total, pltpu.roll(total, 128 - K, 1)), axis=0)
    return t[:, :K], t[:, 2 * K : 3 * K], t[:, 4 * K : 5 * K], t[:, 6 * K : 7 * K]


def kernel(
    rhs_h, near_h, nbr_h, up_h, su_h, fl_h, tr_h, sd_h, dn_h,
    sol_o, res_o,
    rhs_v, near_v, nbr_s, up_v, su_v, fl_s, tr_v, sd_v, dn_v,
    g, hl, hr, s, sw, s2, xb, cst, tst, dst, mg, lg, lf, pg, wg, pc, cf,
    local_sem, near_sem,
    z_send, z_recv, f_send, hl_recv, hr_recv,
    m_send, m_recv, l_send, l_recv, p_send, p_recv, w_send, w_recv,
    c_send, c_recv, o_send, ol_recv, or_recv,
):
    me = lax.axis_index("patch")
    z = lax.axis_index("rhs")
    np_, nz = lax.axis_size("patch"), lax.axis_size("rhs")
    left, right = lax.rem(me + np_ - 1, np_), lax.rem(me + 1, np_)

    def load(i, src, dst):
        copy = pltpu.make_async_copy(src, dst, local_sem.at[i])
        copy.start()
        return copy

    c_rhs = load(0, rhs_h, rhs_v)
    c_up = load(1, up_h, up_v)
    c_su = load(2, su_h, su_v)
    c_nbr = load(3, nbr_h, nbr_s)
    c_fl = load(4, fl_h, fl_s)
    c_tr = load(5, tr_h, tr_v)
    c_sd = load(6, sd_h, sd_v)
    c_dn = load(7, dn_h, dn_v)
    c_near = []
    for p in range(PD):
        copy = pltpu.make_async_copy(near_h.at[p], near_v.at[p], near_sem.at[p])
        copy.start()
        c_near.append(copy)

    barrier = pltpu.get_barrier_semaphore()
    for d in range(1, np_):
        pl.semaphore_signal(barrier, inc=1, device_id=(lax.rem(me + d, np_), z), device_id_type=MESH)
    for d in range(1, nz):
        pl.semaphore_signal(barrier, inc=1, device_id=(me, lax.rem(z + d, nz)), device_id_type=MESH)

    pending = []

    def send(src, dst, ssem, rsem, device):
        copy = pltpu.make_async_remote_copy(
            src_ref=src, dst_ref=dst, send_sem=ssem, recv_sem=rsem, device_id=device, device_id_type=MESH
        )
        copy.start()
        pending.append(copy)

    def arrived(dst, ssem, rsem):
        pltpu.make_async_remote_copy(
            src_ref=dst, dst_ref=dst, send_sem=ssem, recv_sem=rsem, device_id=(right, z), device_id_type=MESH
        ).wait_recv()

    def spread_patch(buf, ssem, rsem):
        for d in range(1, np_):
            to = lax.rem(me + d, np_)
            send(buf.at[me], buf.at[me], ssem.at[d], rsem.at[me], (to, z))

    def gathered_patch(buf, ssem, rsem):
        for d in range(1, np_):
            frm = lax.rem(me + d, np_)
            arrived(buf.at[frm], ssem.at[d], rsem.at[frm])

    c_rhs.wait()
    own_hi, own_lo = [], []
    for p in range(PD):
        hi, lo = split(rhs_v[p])
        g[z, p, 0] = hi
        g[z, p, 1] = lo
        own_hi.append(hi)
        own_lo.append(lo)
    own_hi = jnp.concatenate(own_hi, axis=1)
    own_lo = jnp.concatenate(own_lo, axis=1)

    pl.semaphore_wait(barrier, np_ + nz - 2)

    z_order = (4, 3, 5, 2, 6, 1, 7)
    for d in z_order:
        send(g.at[z], g.at[z], z_send.at[d], z_recv.at[z], (me, lax.rem(z + d, nz)))

    def forward(zz, i):
        send(g.at[zz], hl.at[zz], f_send.at[2 * i], hl_recv.at[zz], (right, z))
        send(g.at[zz], hr.at[zz], f_send.at[2 * i + 1], hr_recv.at[zz], (left, z))

    forward(z, 0)

    c_up.wait()
    c_su.wait()
    for p in range(PD):
        hi, lo = split(dot(su_v[p], up_v[p], NN, HIGH))
        cst[:E, p * W : (p + 1) * W] = hi
        cst[E:, p * W : (p + 1) * W] = lo
    mine = folded(dot(own_hi, cst[...]) + dot(own_lo, cst[...]))
    mg[me] = mine
    spread_patch(mg, m_send, m_recv)

    c_tr.wait()
    for i in range(2):
        a, b = tr_v[0, 2 * i], tr_v[0, 2 * i + 1]
        hi, lo = split(jnp.concatenate((a, b), axis=1))
        tst[:E, i * 128 : (i + 1) * 128] = hi
        tst[E:, i * 128 : (i + 1) * 128] = lo

    c_sd.wait()
    c_dn.wait()
    for p in range(PD):
        hi, lo = split(dot(sd_v[p].T, dn_v[p], NN, HIGH))
        dst[p, :E] = hi
        dst[p, E:] = lo

    for i, d in enumerate((1, 7, 2, 6, 3, 5, 4)):
        zz = lax.rem(z + d, nz)
        arrived(g.at[zz], z_send.at[d], z_recv.at[zz])
        forward(zz, i + 1)

    def assembled(buf, base):
        for zz in range(8):
            for h in range(2):
                for p in range(PD):
                    s[base + p, h, 2 * zz : 2 * zz + 2, :] = buf[zz, p, h]

    assembled(g, PD)

    c_fl.wait()
    gathered_patch(mg, m_send, m_recv)
    src = [fl_s[0, j] for j in range(FL)]
    low2 = lane_of((2, 128)) < E
    chosen = jnp.concatenate(
        (jnp.where(low2, mg[src[0]], mg[src[1]]), jnp.where(low2, mg[src[2]], mg[src[3]])), axis=1
    )
    hi, lo = split(chosen)
    lg[z] = folded(dot(hi, tst[...]) + dot(lo, tst[...]))
    for d in z_order:
        send(lg.at[z], lg.at[z], l_send.at[d], l_recv.at[z], (me, lax.rem(z + d, nz)))

    for d in range(nz):
        zz = lax.rem(z + d, nz)
        arrived(hl.at[zz], f_send.at[0], hl_recv.at[zz])
        arrived(hr.at[zz], f_send.at[0], hr_recv.at[zz])
    assembled(hl, 0)
    assembled(hr, 2 * PD)

    c_nbr.wait()
    first = me * PD - PD
    total_patches = np_ * PD
    ids = [
        [
            jnp.minimum(lax.rem(nbr_s[j, p] - first + 2 * total_patches, total_patches), 3 * PD - 1)
            for j in range(NB)
        ]
        for p in range(PD)
    ]

    for d in range(1, nz):
        zz = lax.rem(z + d, nz)
        arrived(lg.at[zz], l_send.at[d], l_recv.at[zz])
    for zz in range(8):
        lf[2 * zz : 2 * zz + 2, :] = lg[zz]
    local0 = lf[...]

    def image_of(p, pick, lcat):
        blocks = jnp.concatenate([near_v[p, j] for j in range(NB)], axis=1)
        fields = jnp.concatenate([pick(ids[p][j]) for j in range(NB)], axis=1)
        far = dot(lcat, dst[p], NN)
        return dot(blocks, fields).T + (far[:K] + far[K:])

    lcat = jnp.concatenate(split(local0), axis=0)
    for p in range(PD):
        c_near[p].wait()
        hi, lo = split(image_of(p, lambda i: s[i, 0], lcat))
        sw[PD + p, 0] = hi
        sw[PD + p, 1] = lo

    def lanes_joined(ref, base):
        rows = ref.shape[1] * K
        return jnp.concatenate([ref[base + p].reshape(rows, W) for p in range(PD)], axis=1)

    joined_w = lanes_joined(sw, PD)
    pg[me] = packed_grams(jnp.concatenate((lanes_joined(s, PD), joined_w), axis=0))
    spread_patch(pg, p_send, p_recv)
    up_w = dot(joined_w, cst[...])
    up_w = folded(up_w[:K] + up_w[K:])
    low8 = lane_of((8, 128)) < E
    wg[me] = jnp.where(low8, up_w[:8], up_w[8:])
    spread_patch(wg, w_send, w_recv)
    send(sw.at[PD : 2 * PD], sw.at[0:PD], o_send.at[0], ol_recv, (right, z))
    send(sw.at[PD : 2 * PD], sw.at[2 * PD : 3 * PD], o_send.at[1], or_recv, (left, z))

    gathered_patch(pg, p_send, p_recv)
    rr, gg, gt, qq = unpacked_grams(jnp.sum(pg[...], axis=0))
    eye = (lax.broadcasted_iota(jnp.int32, (K, K), 0) == lane_of((K, K))).astype(F32)
    (a1,) = eliminate(0.5 * (gg + gt), rr)
    gtk, inv = eliminate(rr, gt, eye)
    aq = dot(a1, qq, NN, HIGH) - gg
    ka = dot(inv, a1, NN, HIGH)
    ag = dot(a1, gtk, NN, HIGH)
    beta_t = eye - ag + dot(aq, ka, NT, HIGH)
    rr1 = rr - dot(a1, gt, NN, HIGH) + dot(aq, a1, NT, HIGH)

    gathered_patch(wg, w_send, w_recv)
    us = [wg[src[j]] for j in range(FL)]
    rs = [pltpu.roll(u, E, 1) for u in us]
    chosen = jnp.concatenate(
        (
            jnp.concatenate((jnp.where(low8, us[0], rs[1]), jnp.where(low8, rs[0], us[1])), axis=0),
            jnp.concatenate((jnp.where(low8, us[2], rs[3]), jnp.where(low8, rs[2], us[3])), axis=0),
        ),
        axis=1,
    )
    hi, lo = split(chosen)
    local_w = folded(dot(hi, tst[...]) + dot(lo, tst[...]))
    local2 = dot(eye + beta_t, local0, NN, HIGH) - dot(a1, local_w, NN, HIGH)
    lcat = jnp.concatenate(split(local2), axis=0)

    first_co, second_co = eye + beta_t, -a1
    mixer = jnp.concatenate((first_co, first_co, second_co, second_co), axis=1)
    mhi = mixer.astype(BF16).astype(F32)
    mixer = jnp.concatenate((mhi, mixer - mhi), axis=0).astype(BF16)

    arrived(sw.at[0:PD], o_send.at[0], ol_recv)
    arrived(sw.at[2 * PD : 3 * PD], o_send.at[0], or_recv)
    def four(i):
        return jnp.concatenate((s[i].reshape(2 * K, W), sw[i].reshape(2 * K, W)), axis=0)

    for i in range(3 * PD):
        t = dot(mixer, four(i), NN)
        hi, lo = split(t[:K] + t[K:])
        xb[i] = hi
        if PD <= i < 2 * PD:
            s2[i - PD, 0] = hi
            s2[i - PD, 1] = lo

    for p in range(PD):
        hi, lo = split(image_of(p, lambda i: xb[i], lcat))
        s2[p, 2] = hi
        s2[p, 3] = lo

    pc[me] = packed_grams(lanes_joined(s2, 0))
    spread_patch(pc, c_send, c_recv)
    gathered_patch(pc, c_send, c_recv)
    _, gg, gt, _ = unpacked_grams(jnp.sum(pc[...], axis=0))
    (a2,) = eliminate(0.5 * (gg + gt), rr1)
    none = jnp.zeros((K, K), F32)
    cf[:K] = jnp.concatenate((a1, a1, none, none, a2, a2, none, none), axis=1)
    cf[K:] = jnp.concatenate((eye, eye, -a1, -a1, none, none, -a2, -a2), axis=1)
    coeffs = jnp.concatenate((cf[pl.ds(2 * z, 2), :], cf[pl.ds(K + 2 * z, 2), :]), axis=0)
    chi = coeffs.astype(BF16).astype(F32)
    coeffs = jnp.concatenate((chi, coeffs - chi), axis=0).astype(BF16)
    for p in range(PD):
        t = dot(coeffs, jnp.concatenate((four(PD + p), s2[p].reshape(4 * K, W)), axis=0), NN)
        t = t[:4] + t[4:]
        sol_o[p] = t[:2]
        res_o[p] = t[2:]

    for copy in pending:
        copy.wait_send()


def on_device(*args):
    args = list(args)
    args[2] = args[2].T
    args[8] = jnp.swapaxes(args[8], 1, 2)
    np_, nz = lax.axis_size("patch"), lax.axis_size("rhs")
    vm = pltpu.VMEM
    sem = pltpu.SemaphoreType.DMA
    scratch = [
        vm((PD, 2, W), F32),
        vm((PD, NB, W, W), BF16),
        pltpu.SMEM((NB, PD), jnp.int32),
        vm((PD, E, W), F32),
        vm((PD, E, E), F32),
        pltpu.SMEM((1, FL), jnp.int32),
        vm((1, FL, E, E), F32),
        vm((PD, E, E), F32),
        vm((PD, E, W), F32),
        vm((nz, PD, 2, 2, W), BF16),
        vm((nz, PD, 2, 2, W), BF16),
        vm((nz, PD, 2, 2, W), BF16),
        vm((3 * PD, 2, K, W), BF16),
        vm((3 * PD, 2, K, W), BF16),
        vm((PD, 4, K, W), BF16),
        vm((3 * PD, K, W), BF16),
        vm((2 * E, PD * W), BF16),
        vm((2 * E, FL * E), BF16),
        vm((PD, 2 * E, W), BF16),
        vm((np_, 2, 128), F32),
        vm((nz, 2, 128), F32),
        vm((K, 128), F32),
        vm((np_, 8, 128), F32),
        vm((np_, 8, 128), F32),
        vm((np_, 8, 128), F32),
        vm((2 * K, 128), F32),
        sem((8,)), sem((PD,)),
        sem((nz,)), sem((nz,)), sem((2 * nz,)), sem((nz,)), sem((nz,)),
        sem((np_,)), sem((np_,)), sem((nz,)), sem((nz,)),
        sem((np_,)), sem((np_,)), sem((np_,)), sem((np_,)),
        sem((np_,)), sem((np_,)), sem((2,)), sem(()), sem(()),
    ]
    any_spec = pl.BlockSpec(memory_space=pltpu.MemorySpace.HBM)
    vmem_spec = pl.BlockSpec(memory_space=pltpu.VMEM)
    out = jax.ShapeDtypeStruct((PD, 2, W), F32)
    return pl.pallas_call(
        kernel,
        out_shape=(out, out),
        in_specs=[any_spec] * 9,
        out_specs=(vmem_spec, vmem_spec),
        scratch_shapes=scratch,
        compiler_params=pltpu.CompilerParams(
            collective_id=0, has_side_effects=True, vmem_limit_bytes=66_000_000
        ),
    )(*args)


def solution(mesh):
    return jax.shard_map(
        on_device,
        mesh=mesh,
        in_specs=(
            P("patch", "rhs", None),
            P("patch", None, None, None),
            P("patch", None),
            P("patch", None, None),
            P("patch", None, None),
            P("patch", None),
            P("patch", None, None, None),
            P("patch", None, None),
            P("patch", None, None),
        ),
        out_specs=(P("patch", "rhs", None), P("patch", "rhs", None)),
        check_vma=False,
    )
```

time: 140 us -> 55.3 us (0.39)
  Pallas kernels: 0 us -> 51.7 us
  starting transfers between devices: 51.4 us -> 0 us
  waiting for transfers between devices: 33 us -> 0 us
  matrix products: 24.7 us -> 0 us
  other arithmetic: 19.1 us -> 0 us
  local copies, waits for them, and re-layouts: 9.85 us -> 2.7 us
    pallas_call x0 -> x1, Pallas kernels: none -> 51.7 us  [on_device(): pl.pallas_call(kernel, out_shape=(out, out), in_specs=[any_spec] * 9, out...]
    all_to_all x7 -> x0, starting transfers between devices: 45.8 us -> none  [from_everyone(): lax.all_to_all(jnp.broadcast_to(array[None], (devices, *array.shape)), ax...]
    all_to_all x7 -> x0, waiting for transfers between devices: 33 us -> none  [from_everyone(): lax.all_to_all(jnp.broadcast_to(array[None], (devices, *array.shape)), ax...]
    dot_general x23 -> x0, matrix products: 23.5 us -> none  [the longest x2 12.5 us: apply_operator(): jnp.einsum('pjvw,pjkw->pkv', near_blocks, picked, preferred_element_type=...]
    another operation x15 -> x0, other arithmetic: 12 us -> none  [the longest x9 6.4 us: spd_solve(): factor = jnp.linalg.cholesky(matrix)]
    ppermute x4 -> x0, starting transfers between devices: 5.52 us -> none  [the longest x2 2.98 us: with_halo(): lax.ppermute(lax.slice_in_dim(block, 0, width, axis=dim), axis, backward)]
    all_to_all x6 -> x0, other arithmetic: 4.8 us -> none  [from_everyone(): lax.all_to_all(jnp.broadcast_to(array[None], (devices, *array.shape)), ax...]
    unnamed x24 -> x2, local copies, waits for them, and re-layouts: 5.38 us -> 2.7 us
  transfers between devices with their start and end apart: 11 -> 0, of which waited for: 6 -> 0; matrix products, arithmetic and copies ran while one was open for 20% -> 0% of each run, Pallas kernels for 0% -> 0%
where the time goes in v1:
time: 55.3 us; the launch traced here: 55.1 us
  Pallas kernels  51.7 us (93%)
  local copies, waits for them, and re-layouts  2.7 us (5%)
  between operations  0.64 us (1%)
    pallas_call x1, Pallas kernels, on_device(): pl.pallas_call(kernel, out_shape=(out, out), in_specs=[any_spec] * 9, out...  51.7 us
    unnamed x2, local copies, waits for them, and re-layouts  2.7 us

profile of v1, /device:TPU:1, one launch (start us, length us, event | category | flops | bytes accessed | tf_op | source)
XLA Modules:
  0.0 55.1 jit_solution(4257119760864201274)
XLA Ops:
  0.6 51.7 %shard_map.104 = (f32[8,2,384]{2,1,0:T(2,128)}, f32[8,2,384]{2,1,0:T(2,128)}) custom-call(f32[8,2,384]{2,1,0:T(2,128)} %rhs_h.1, bf16[8,4,384,384]{3,2,1,0:T(8,128)(2,1)} %near_h.1, s32[4,8]{1,0:T(4,128)} %bitcast.3, f32[8,64,384]{2,1,0:T(8,128)} %up_h.1, f32[8,64,64]{2,1,0:T(8,128)} %su_h.1, s32[1,4]{1,0:T(1,128)} %fl_h.1, f32[1,4,64,64]{3,2,1,0:T(8,128)} %tr_h.1, ...), custom_call_target="tpu_custom_call" | custom-call | tf_op jit(solution)/shard_map/pallas_call | solution.py:367
  52.4 1.4 %copy.13 = f32[8,2,384]{2,1,0:T(2,128)} copy(f32[8,2,384]{2,1,0:T(2,128)} %get-tuple-element.4) | data formatting | bytes 49152
  53.7 1.4 %copy.14 = f32[8,2,384]{2,1,0:T(2,128)} copy(f32[8,2,384]{2,1,0:T(2,128)} %get-tuple-element.5) | data formatting | bytes 49152

commit v2 on v1

v2 whole, which is shorter than its diff:
```python
import jax
import jax.numpy as jnp
from jax import lax
from jax.experimental import pallas as pl
from jax.experimental.pallas import tpu as pltpu
from jax.sharding import PartitionSpec as P

F32 = jnp.float32
BF16 = jnp.bfloat16
HIGH = lax.Precision.HIGHEST
MESH = pl.DeviceIdType.MESH
PD, K, W, E, NB, FL = 8, 16, 384, 64, 4, 4
NT = (((1,), (1,)), ((), ()))
NN = (((1,), (0,)), ((), ()))


def dot(a, b, dims=NT, precision=None):
    return lax.dot_general(a, b, dims, precision=precision, preferred_element_type=F32)


def split(x):
    hi = x.astype(BF16)
    return hi, (x - hi.astype(F32)).astype(BF16)


def folded(x):
    return x + pltpu.roll(x, 64, 1)


def lane_of(shape):
    return lax.broadcasted_iota(jnp.int32, shape, 1)


def eliminate(top, *others):
    a = jnp.concatenate((top, *others), axis=0)
    lanes = lane_of(a.shape)
    group = 4
    for base in range(0, K, group):
        columns = [jnp.broadcast_to(a[:, k : k + 1], a.shape) for k in range(base, base + group)]
        for i in range(group):
            k = base + i
            column = columns[i]
            inverse = 1.0 / column[k : k + 1, :]
            scaled = column * inverse
            for j in range(i + 1, group):
                columns[j] = columns[j] - scaled * columns[j][k : k + 1, :]
            a = jnp.where(lanes == k, scaled, a - scaled * a[k : k + 1, :])
    return a[K:]


def packed_grams(stack):
    full = dot(stack, stack)
    full = jnp.concatenate((full, jnp.zeros((4 * K, 128 - 4 * K), F32)), axis=1)

    def half(top, low):
        t = top + low
        t = t + pltpu.roll(t, 128 - K, 1)
        even = (lane_of((8, 128)) // K) % 2 == 0
        return jnp.where(even, t[:8], pltpu.roll(t[8:], K, 1))

    a = half(full[:K], full[K : 2 * K])
    b = half(full[2 * K : 3 * K], full[3 * K :])
    return jnp.where(lane_of((8, 128)) < 4 * K, a, pltpu.roll(b, 4 * K, 1))


def unpacked_grams(total):
    t = jnp.concatenate((total, pltpu.roll(total, 128 - K, 1)), axis=0)
    return t[:, :K], t[:, 2 * K : 3 * K], t[:, 4 * K : 5 * K], t[:, 6 * K : 7 * K]


def far_first():
    order = [(dy, dx, dc) for dy in range(4) for dx in range(4) for dc in range(2)]
    order.remove((0, 0, 0))
    return sorted(order, key=lambda t: -(min(t[0], 4 - t[0]) + min(t[1], 4 - t[1])))


def product_split(left, right):
    rhi, rlo = split(right)
    twice = jnp.concatenate((left, left), axis=1)
    hi = twice.astype(BF16)
    lo = (twice - hi.astype(F32)).astype(BF16)
    t = dot(jnp.concatenate((hi, lo), axis=0), jnp.concatenate((rhi, rlo), axis=0), NN)
    return split(t[:E] + t[E:])


def kernel(
    rhs_h, near_h, nbr_h, up_h, su_h, fl_h, tr_h, sd_h, dn_h,
    both_o,
    rhs_v, near_v, nbr_s, up_v, su_v, fl_s, tr_v, sd_v, dn_v,
    gh, gl, hlh, hrh, sh, sl, wh, wl, d2h, d2l, imh, iml, nf,
    cst, tst, dst, mg, lg, lf, pg, wg, pc, cf,
    local_sem, z_recv, sends, recvs,
):
    me = lax.axis_index("patch")
    z = lax.axis_index("rhs")
    np_, nz = lax.axis_size("patch"), lax.axis_size("rhs")
    left, right = lax.rem(me + np_ - 1, np_), lax.rem(me + 1, np_)
    core, chip = lax.rem(me, 2), me // 2
    cx, cy = lax.rem(chip, 4), chip // 4
    peers = [
        (lax.rem(cy + dy, 4) * 4 + lax.rem(cx + dx, 4)) * 2 + lax.rem(core + dc, 2)
        for dy, dx, dc in far_first()
    ]
    z_order = (4, 3, 5, 2, 6, 1, 7)
    z_peers = [lax.rem(z + d, nz) for d in z_order]

    def load(i, src, dst):
        copy = pltpu.make_async_copy(src, dst, local_sem.at[i])
        copy.start()
        return copy

    c_rhs = load(0, rhs_h, rhs_v)
    barrier = pltpu.get_barrier_semaphore()
    for to in z_peers:
        pl.semaphore_signal(barrier, inc=1, device_id=(me, to), device_id_type=MESH)
    for to in peers:
        pl.semaphore_signal(barrier, inc=1, device_id=(to, z), device_id_type=MESH)
    c_up = load(1, up_h, up_v)
    c_su = load(2, su_h, su_v)
    c_tr = load(5, tr_h, tr_v)
    c_sd = load(6, sd_h, sd_v)
    c_dn = load(7, dn_h, dn_v)
    c_fl = load(4, fl_h, fl_s)
    c_nbr = load(3, nbr_h, nbr_s)
    c_near = load(8, near_h, near_v)

    M, L, PA, WA, PC, ZH, ZL, HL, HR, OL, OR, WL, WR, WLL, WRL = range(15)

    def send(src, dst, kind, device, recv=None):
        pltpu.make_async_remote_copy(
            src_ref=src,
            dst_ref=dst,
            send_sem=sends.at[kind],
            recv_sem=recvs.at[kind] if recv is None else recv,
            device_id=device,
            device_id_type=MESH,
        ).start()

    def handle(ref, kind, recv=None):
        return pltpu.make_async_remote_copy(
            src_ref=ref,
            dst_ref=ref,
            send_sem=sends.at[kind],
            recv_sem=recvs.at[kind] if recv is None else recv,
            device_id=(right, z),
            device_id_type=MESH,
        )

    def spread_patch(buf, kind):
        for to in peers:
            send(buf.at[me], buf.at[me], kind, (to, z))

    def gathered_patch(buf, kind):
        handle(buf.at[pl.ds(0, np_ - 1)], kind).wait_recv()

    def spread_z(buf, kind, recv=None):
        for to in z_peers:
            send(buf.at[z], buf.at[z], kind, (me, to), recv)

    def forward(zz):
        send(gh.at[zz], hlh.at[zz], HL, (right, z))
        send(gh.at[zz], hrh.at[zz], HR, (left, z))

    c_rhs.wait()
    own_hi, own_lo = [], []
    for p in range(PD):
        hi, lo = split(rhs_v[p])
        gh[z, p] = hi
        gl[z, p] = lo
        own_hi.append(hi)
        own_lo.append(lo)
    own_hi = jnp.concatenate(own_hi, axis=1)
    own_lo = jnp.concatenate(own_lo, axis=1)

    pl.semaphore_wait(barrier, np_ + nz - 2)
    spread_z(gh, ZH, z_recv.at[z])
    forward(z)

    c_up.wait()
    c_su.wait()
    for p in range(PD):
        hi, lo = product_split(su_v[p], up_v[p])
        cst[:E, p * W : (p + 1) * W] = hi
        cst[E:, p * W : (p + 1) * W] = lo
    mg[me] = folded(dot(own_hi, cst[...]) + dot(own_lo, cst[...]))
    spread_patch(mg, M)

    def take(d):
        zz = lax.rem(z + d, nz)
        handle(gh.at[zz], ZH, z_recv.at[zz]).wait_recv()
        forward(zz)

    for d in (1, 7, 2, 6):
        take(d)

    c_tr.wait()
    for i in range(2):
        hi, lo = split(jnp.concatenate((tr_v[0, 2 * i], tr_v[0, 2 * i + 1]), axis=1))
        tst[:E, i * 128 : (i + 1) * 128] = hi
        tst[E:, i * 128 : (i + 1) * 128] = lo
    c_sd.wait()
    c_dn.wait()
    for p in range(PD):
        hi, lo = product_split(sd_v[p].T, dn_v[p])
        dst[p, :E] = hi
        dst[p, E:] = lo

    for d in (3, 5, 4):
        take(d)
    spread_z(gl, ZL)

    def assembled(buf, dest, base):
        for zz in range(8):
            for p in range(PD):
                dest[base + p, 2 * zz : 2 * zz + 2, :] = buf[zz, p]

    assembled(gh, sh, PD)

    c_fl.wait()
    src = [fl_s[0, j] for j in range(FL)]
    gathered_patch(mg, M)
    low2 = lane_of((2, 128)) < E
    chosen = jnp.concatenate(
        (jnp.where(low2, mg[src[0]], mg[src[1]]), jnp.where(low2, mg[src[2]], mg[src[3]])), axis=1
    )
    hi, lo = split(chosen)
    lg[z] = folded(dot(hi, tst[...]) + dot(lo, tst[...]))
    spread_z(lg, L)

    handle(hlh, HL).wait_recv()
    assembled(hlh, sh, 0)
    handle(hrh, HR).wait_recv()
    assembled(hrh, sh, 2 * PD)

    c_nbr.wait()
    first = me * PD - PD
    total_patches = np_ * PD
    ids = [
        [
            jnp.minimum(lax.rem(nbr_s[j, p] - first + 2 * total_patches, total_patches), 3 * PD - 1)
            for j in range(NB)
        ]
        for p in range(PD)
    ]
    c_near.wait()

    def near_of(p, field):
        blocks = jnp.concatenate([near_v[p, j] for j in range(NB)], axis=1)
        picked = jnp.concatenate([field[ids[p][j]] for j in range(NB)], axis=1)
        return dot(blocks, picked).T

    def far_of(p, lcat):
        far = dot(lcat, dst[p], NN)
        return far[:K] + far[K:]

    for p in range(PD):
        nf[p] = near_of(p, sh)

    handle(gl.at[pl.ds(0, nz - 1)], ZL).wait_recv()
    assembled(gl, sl, PD)
    mid = pl.ds(PD, PD)
    send(sl.at[mid], sl.at[pl.ds(0, PD)], OL, (right, z))
    send(sl.at[mid], sl.at[pl.ds(2 * PD, PD)], OR, (left, z))

    handle(lg.at[pl.ds(0, nz - 1)], L).wait_recv()
    for zz in range(8):
        lf[2 * zz : 2 * zz + 2, :] = lg[zz]
    local0 = lf[...]
    lcat = jnp.concatenate(split(local0), axis=0)
    for p in range(PD):
        hi, lo = split(nf[p] + far_of(p, lcat))
        wh[PD + p] = hi
        wl[PD + p] = lo

    def joined(base, *refs):
        return jnp.concatenate(
            [jnp.concatenate([ref[base + p] for p in range(PD)], axis=1) for ref in refs], axis=0
        )

    pg[me] = packed_grams(joined(PD, sh, sl, wh, wl))
    spread_patch(pg, PA)
    up_w = dot(joined(PD, wh, wl), cst[...])
    up_w = folded(up_w[:K] + up_w[K:])
    low8 = lane_of((8, 128)) < E
    wg[me] = jnp.where(low8, up_w[:8], up_w[8:])
    spread_patch(wg, WA)
    send(wh.at[mid], wh.at[pl.ds(0, PD)], WL, (right, z))
    send(wh.at[mid], wh.at[pl.ds(2 * PD, PD)], WR, (left, z))
    send(wl.at[mid], wl.at[pl.ds(0, PD)], WLL, (right, z))
    send(wl.at[mid], wl.at[pl.ds(2 * PD, PD)], WRL, (left, z))

    gathered_patch(pg, PA)
    rr, gg, gt, qq = unpacked_grams(jnp.sum(pg[...], axis=0))
    eye = (lax.broadcasted_iota(jnp.int32, (K, K), 0) == lane_of((K, K))).astype(F32)
    a1 = eliminate(0.5 * (gg + gt), rr)
    both = eliminate(rr, gt, eye)
    gtk, inv = both[:K], both[K:]
    aq = dot(a1, qq, NN, HIGH) - gg
    ka = dot(inv, a1, NN, HIGH)
    ag = dot(a1, gtk, NN, HIGH)
    first_co, second_co = 2.0 * eye - ag + dot(aq, ka, NT, HIGH), -a1
    rr1 = rr - dot(a1, gt, NN, HIGH) + dot(aq, a1, NT, HIGH)
    mixer = jnp.concatenate((first_co, first_co, second_co, second_co), axis=1)
    mhi = mixer.astype(BF16).astype(F32)
    mixer = jnp.concatenate((mhi, mixer - mhi), axis=0).astype(BF16)

    gathered_patch(wg, WA)
    for kind, ref, base in (
        (OL, sl, 0), (OR, sl, 2 * PD), (WL, wh, 0), (WR, wh, 2 * PD), (WLL, wl, 0), (WRL, wl, 2 * PD)
    ):
        handle(ref.at[pl.ds(base, PD)], kind).wait_recv()

    us = [wg[src[j]] for j in range(FL)]
    rs = [pltpu.roll(u, E, 1) for u in us]
    chosen = jnp.concatenate(
        (
            jnp.concatenate((jnp.where(low8, us[0], rs[1]), jnp.where(low8, rs[0], us[1])), axis=0),
            jnp.concatenate((jnp.where(low8, us[2], rs[3]), jnp.where(low8, rs[2], us[3])), axis=0),
        ),
        axis=1,
    )
    hi, lo = split(chosen)
    local_w = folded(dot(hi, tst[...]) + dot(lo, tst[...]))
    local2 = dot(first_co, local0, NN, HIGH) + dot(second_co, local_w, NN, HIGH)
    lcat = jnp.concatenate(split(local2), axis=0)

    for i in range(3 * PD):
        t = dot(mixer, jnp.concatenate((sh[i], sl[i], wh[i], wl[i]), axis=0), NN)
        hi, lo = split(t[:K] + t[K:])
        d2h[i] = hi
        if PD <= i < 2 * PD:
            d2l[i - PD] = lo

    for p in range(PD):
        hi, lo = split(near_of(p, d2h) + far_of(p, lcat))
        imh[p] = hi
        iml[p] = lo

    wide = [jnp.concatenate([ref[b + p] for p in range(PD)], axis=1) for ref, b in ((d2h, PD), (d2l, 0), (imh, 0), (iml, 0))]
    pc[me] = packed_grams(jnp.concatenate(wide, axis=0))
    spread_patch(pc, PC)

    cf[0:K, 0:K] = a1
    cf[K : 2 * K, 0:K] = rr1
    mine_a1, mine_rr1 = cf[pl.ds(2 * z, 2), 0:K], cf[pl.ds(K + 2 * z, 2), 0:K]
    cf[2 * K : 3 * K, 0:K] = eye
    mine_eye = cf[pl.ds(2 * K + 2 * z, 2), 0:K]
    none = jnp.zeros((2, K), F32)
    coeffs = jnp.concatenate(
        (
            jnp.concatenate((mine_a1, mine_a1, none, none), axis=1),
            jnp.concatenate((mine_eye, mine_eye, -mine_a1, -mine_a1), axis=1),
        ),
        axis=0,
    )
    chi = coeffs.astype(BF16).astype(F32)
    coeffs = jnp.concatenate((chi, coeffs - chi), axis=0).astype(BF16)
    for p in range(PD):
        q = PD + p
        t = dot(coeffs, jnp.concatenate((sh[q], sl[q], wh[q], wl[q]), axis=0), NN)
        both_o[p] = t[:4] + t[4:]
    rows8 = jnp.concatenate((mine_rr1,) * 4, axis=0)
    row8 = lax.broadcasted_iota(jnp.int32, (8, 4 * K), 0)
    lane8 = lane_of((8, 4 * K)) < 2 * K
    is_sol = lax.rem(row8, 4) < 2
    sign = jnp.where(is_sol, jnp.where(lane8, 1.0, 0.0), jnp.where(lane8, 0.0, -1.0))

    gathered_patch(pc, PC)
    _, gg, gt, _ = unpacked_grams(jnp.sum(pc[...], axis=0))
    a2 = eliminate(0.5 * (gg + gt), rows8)
    a2 = jnp.concatenate((a2, a2, a2, a2), axis=1)
    chi = a2.astype(BF16).astype(F32)
    coeffs = (jnp.where(row8 < 4, chi, a2 - chi) * sign).astype(BF16)
    for p in range(PD):
        t = dot(coeffs, jnp.concatenate((d2h[PD + p], d2l[p], imh[p], iml[p]), axis=0), NN)
        both_o[p] += t[:4] + t[4:]

    for ref, kind in ((mg, M), (pg, PA), (wg, WA), (pc, PC)):
        handle(ref.at[pl.ds(0, np_ - 1)], kind).wait_send()
    for ref, kind in ((lg, L), (gh, ZH), (gl, ZL)):
        handle(ref.at[pl.ds(0, nz - 1)], kind).wait_send()
    for ref, kind in ((hlh, HL), (hrh, HR)):
        handle(ref, kind).wait_send()
    for ref, kind in ((sl, OL), (sl, OR), (wh, WL), (wh, WR), (wl, WLL), (wl, WRL)):
        handle(ref.at[mid], kind).wait_send()


def on_device(*args):
    args = list(args)
    args[2] = args[2].T
    args[8] = jnp.swapaxes(args[8], 1, 2)
    args = [pltpu.with_memory_space_constraint(x, pltpu.HBM) for x in args]
    np_, nz = lax.axis_size("patch"), lax.axis_size("rhs")
    vm = pltpu.VMEM
    sem = pltpu.SemaphoreType.DMA
    chunks = vm((nz, PD, 2, W), BF16)
    three = vm((3 * PD, K, W), BF16)
    one = vm((PD, K, W), BF16)
    message = vm((np_, 8, 128), F32)
    scratch = [
        vm((PD, 2, W), F32),
        vm((PD, NB, W, W), BF16),
        pltpu.SMEM((NB, PD), jnp.int32),
        vm((PD, E, W), F32),
        vm((PD, E, E), F32),
        pltpu.SMEM((1, FL), jnp.int32),
        vm((1, FL, E, E), F32),
        vm((PD, E, E), F32),
        vm((PD, E, W), F32),
        chunks, chunks, chunks, chunks,
        three, three, three, three, three, one, one, one,
        vm((PD, K, W), F32),
        vm((2 * E, PD * W), BF16),
        vm((2 * E, FL * E), BF16),
        vm((PD, 2 * E, W), BF16),
        vm((np_, 2, 128), F32),
        vm((nz, 2, 128), F32),
        vm((K, 128), F32),
        message, message, message,
        vm((3 * K, 128), F32),
        sem((9,)), sem((nz,)), sem((15,)), sem((15,)),
    ]
    out = pl.pallas_call(
        kernel,
        out_shape=pltpu.VMEM((PD, 4, W), F32),
        in_specs=[pl.BlockSpec(memory_space=pltpu.MemorySpace.HBM)] * 9,
        out_specs=pl.BlockSpec(memory_space=pltpu.VMEM),
        scratch_shapes=scratch,
        compiler_params=pltpu.CompilerParams(
            collective_id=0, has_side_effects=True, vmem_limit_bytes=60_000_000
        ),
    )(*args)
    return out[:, :2], out[:, 2:]


def solution(mesh):
    return jax.shard_map(
        on_device,
        mesh=mesh,
        in_specs=(
            P("patch", "rhs", None),
            P("patch", None, None, None),
            P("patch", None),
            P("patch", None, None),
            P("patch", None, None),
            P("patch", None),
            P("patch", None, None, None),
            P("patch", None, None),
            P("patch", None, None),
        ),
        out_specs=(P("patch", "rhs", None), P("patch", "rhs", None)),
        check_vma=False,
    )
```

time: 55.3 us -> 42.1 us (0.76)
  Pallas kernels: 51.7 us -> 40.7 us
  local copies, waits for them, and re-layouts: 2.7 us -> 0.64 us
    pallas_call x1, Pallas kernels: 51.7 us -> 40.7 us  [on_device(): pl.pallas_call(kernel, out_shape=pltpu.VMEM((PD, 4, W), F32), in_specs=[p...]
    unnamed x2 -> x0, local copies, waits for them, and re-layouts: 2.7 us -> none
    slice x0 -> x1, local copies, waits for them, and re-layouts: none -> 0.64 us  [on_device(): return (out[:, :2], out[:, 2:])]
where the time goes in v2:
time: 42.1 us; the launch traced here: 42 us
  Pallas kernels  40.7 us (97%)
  local copies, waits for them, and re-layouts  0.64 us (2%)
  between operations  0.64 us (2%)
    pallas_call x1, Pallas kernels, on_device(): pl.pallas_call(kernel, out_shape=pltpu.VMEM((PD, 4, W), F32), in_specs=[p...  40.7 us

profile of v2, /device:TPU:1, one launch (start us, length us, event | category | flops | bytes accessed | tf_op | source)
XLA Modules:
  0.0 42.0 jit_solution(2926677217425230907)
XLA Ops:
  0.6 40.7 %shard_map.104 = f32[8,4,384]{2,1,0:T(4,128)S(1)} custom-call(f32[8,2,384]{2,1,0:T(2,128)} %rhs_h.1, bf16[8,4,384,384]{3,2,1,0:T(8,128)(2,1)} %near_h.1, s32[4,8]{1,0:T(4,128)} %bitcast.3, f32[8,64,384]{2,1,0:T(8,128)} %up_h.1, f32[8,64,64]{2,1,0:T(8,128)} %su_h.1, s32[1,4]{1,0:T(1,128)} %fl_h.1, f32[1,4,64,64]{3,2,1,0:T(8,128)} %tr_h.1, f32[8,64,64]{2,1,0:T(8,128)} %sd_h.1, ...), custom_call_target="tpu_custom_call" | custom-call | tf_op jit(solution)/shard_map/pallas_call | solution.py:423
  41.4 0.6 %fusion = (f32[8,2,384]{2,1,0:T(2,128)}, f32[8,2,384]{2,1,0:T(2,128)}) fusion(f32[8,4,384]{2,1,0:T(4,128)S(1)} %shard_map.104), kind=kLoop, calls=%fused_computation | loop fusion | bytes 98304 | tf_op jit(solution)/shard_map/slice | solution.py:433

commit v3 on v2

--- a/solution.py
+++ b/solution.py
@@ -48,24 +48,21 @@
     return a[K:]
 
 
-def packed_grams(stack):
-    full = dot(stack, stack)
-    full = jnp.concatenate((full, jnp.zeros((4 * K, 128 - 4 * K), F32)), axis=1)
-
-    def half(top, low):
-        t = top + low
-        t = t + pltpu.roll(t, 128 - K, 1)
-        even = (lane_of((8, 128)) // K) % 2 == 0
-        return jnp.where(even, t[:8], pltpu.roll(t[8:], K, 1))
-
-    a = half(full[:K], full[K : 2 * K])
-    b = half(full[2 * K : 3 * K], full[3 * K :])
-    return jnp.where(lane_of((8, 128)) < 4 * K, a, pltpu.roll(b, 4 * K, 1))
+def packed_grams(rows, high, low):
+    full = dot(rows, high) + dot(rows, low)
+    a = full[:K] + full[K : 2 * K]
+    b = full[2 * K : 3 * K] + full[3 * K :]
+    return jnp.concatenate((a[:8], a[8:], b[:8], b[8:]), axis=1)
 
 
 def unpacked_grams(total):
-    t = jnp.concatenate((total, pltpu.roll(total, 128 - K, 1)), axis=0)
-    return t[:, :K], t[:, 2 * K : 3 * K], t[:, 4 * K : 5 * K], t[:, 6 * K : 7 * K]
+    def at(lane):
+        return pltpu.roll(total, 128 - lane, 1) if lane else total
+
+    def block(lane):
+        return jnp.concatenate((at(lane), at(lane + 2 * K)), axis=0)[:, :K]
+
+    return block(0), block(K), block(4 * K), block(5 * K)
 
 
 def far_first():
@@ -87,7 +84,7 @@
     rhs_h, near_h, nbr_h, up_h, su_h, fl_h, tr_h, sd_h, dn_h,
     both_o,
     rhs_v, near_v, nbr_s, up_v, su_v, fl_s, tr_v, sd_v, dn_v,
-    gh, gl, hlh, hrh, sh, sl, wh, wl, d2h, d2l, imh, iml, nf,
+    gh, gl, hlh, hrh, sh, sl, wh, wl, d2h, d2w, imh, iml, nf,
     cst, tst, dst, mg, lg, lf, pg, wg, pc, cf,
     local_sem, z_recv, sends, recvs,
 ):
@@ -122,8 +119,6 @@
     c_dn = load(7, dn_h, dn_v)
     c_fl = load(4, fl_h, fl_s)
     c_nbr = load(3, nbr_h, nbr_s)
-    c_near = load(8, near_h, near_v)
-
     M, L, PA, WA, PC, ZH, ZL, HL, HR, OL, OR, WL, WR, WLL, WRL = range(15)
 
     def send(src, dst, kind, device, recv=None):
@@ -178,6 +173,7 @@
 
     c_up.wait()
     c_su.wait()
+    c_near = load(8, near_h, near_v)
     for p in range(PD):
         hi, lo = product_split(su_v[p], up_v[p])
         cst[:E, p * W : (p + 1) * W] = hi
@@ -190,31 +186,19 @@
         handle(gh.at[zz], ZH, z_recv.at[zz]).wait_recv()
         forward(zz)
 
-    for d in (1, 7, 2, 6):
-        take(d)
-
     c_tr.wait()
     for i in range(2):
         hi, lo = split(jnp.concatenate((tr_v[0, 2 * i], tr_v[0, 2 * i + 1]), axis=1))
         tst[:E, i * 128 : (i + 1) * 128] = hi
         tst[E:, i * 128 : (i + 1) * 128] = lo
-    c_sd.wait()
-    c_dn.wait()
-    for p in range(PD):
-        hi, lo = product_split(sd_v[p].T, dn_v[p])
-        dst[p, :E] = hi
-        dst[p, E:] = lo
-
-    for d in (3, 5, 4):
+
+    for d in (1, 7, 2, 6, 3, 5, 4):
         take(d)
-    spread_z(gl, ZL)
 
     def assembled(buf, dest, base):
         for zz in range(8):
             for p in range(PD):
                 dest[base + p, 2 * zz : 2 * zz + 2, :] = buf[zz, p]
-
-    assembled(gh, sh, PD)
 
     c_fl.wait()
     src = [fl_s[0, j] for j in range(FL)]
@@ -226,6 +210,19 @@
     hi, lo = split(chosen)
     lg[z] = folded(dot(hi, tst[...]) + dot(lo, tst[...]))
     spread_z(lg, L)
+    spread_z(gl, ZL)
+
+    assembled(gh, sh, PD)
+    c_sd.wait()
+    c_dn.wait()
+    for p in range(PD):
+        hi, lo = product_split(sd_v[p].T, dn_v[p])
+        dst[p, :E] = hi
+        dst[p, E:] = lo
+
+    c_near.wait()
+    for p in range(PD):
+        nf[p] = dot(near_v[p, 0], sh[PD + p]).T
 
     handle(hlh, HL).wait_recv()
     assembled(hlh, sh, 0)
@@ -242,11 +239,10 @@
         ]
         for p in range(PD)
     ]
-    c_near.wait()
-
-    def near_of(p, field):
-        blocks = jnp.concatenate([near_v[p, j] for j in range(NB)], axis=1)
-        picked = jnp.concatenate([field[ids[p][j]] for j in range(NB)], axis=1)
+
+    def near_of(p, field, start):
+        blocks = jnp.concatenate([near_v[p, j] for j in range(start, NB)], axis=1)
+        picked = jnp.concatenate([field[ids[p][j]] for j in range(start, NB)], axis=1)
         return dot(blocks, picked).T
 
     def far_of(p, lcat):
@@ -254,7 +250,7 @@
         return far[:K] + far[K:]
 
     for p in range(PD):
-        nf[p] = near_of(p, sh)
+        nf[p] += near_of(p, sh, 1)
 
     handle(gl.at[pl.ds(0, nz - 1)], ZL).wait_recv()
     assembled(gl, sl, PD)
@@ -277,7 +273,7 @@
             [jnp.concatenate([ref[base + p] for p in range(PD)], axis=1) for ref in refs], axis=0
         )
 
-    pg[me] = packed_grams(joined(PD, sh, sl, wh, wl))
+    pg[me] = packed_grams(joined(PD, sh, sl, wh, wl), joined(PD, wh, sh), joined(PD, wl, sl))
     spread_patch(pg, PA)
     up_w = dot(joined(PD, wh, wl), cst[...])
     up_w = folded(up_w[:K] + up_w[K:])
@@ -290,17 +286,22 @@
     send(wl.at[mid], wl.at[pl.ds(2 * PD, PD)], WRL, (left, z))
 
     gathered_patch(pg, PA)
-    rr, gg, gt, qq = unpacked_grams(jnp.sum(pg[...], axis=0))
+    gg, rr, qq, gt = unpacked_grams(jnp.sum(pg[...], axis=0))
     eye = (lax.broadcasted_iota(jnp.int32, (K, K), 0) == lane_of((K, K))).astype(F32)
     a1 = eliminate(0.5 * (gg + gt), rr)
-    both = eliminate(rr, gt, eye)
-    gtk, inv = both[:K], both[K:]
+    inv = eliminate(rr, eye)
+    blank = jnp.zeros((2 * K, K), F32)
     aq = dot(a1, qq, NN, HIGH) - gg
+    ag = dot(a1, gg, NT, HIGH)
     ka = dot(inv, a1, NN, HIGH)
-    ag = dot(a1, gtk, NN, HIGH)
-    first_co, second_co = 2.0 * eye - ag + dot(aq, ka, NT, HIGH), -a1
-    rr1 = rr - dot(a1, gt, NN, HIGH) + dot(aq, a1, NT, HIGH)
-    mixer = jnp.concatenate((first_co, first_co, second_co, second_co), axis=1)
+    row16, lane64 = lax.broadcasted_iota(jnp.int32, (K, 4 * K), 0), lane_of((K, 4 * K))
+    twice = jnp.where((lane64 == row16) | (lane64 == row16 + K), 2.0, 0.0)
+    minus = jnp.concatenate((jnp.zeros((K, 2 * K), F32), -a1, -a1), axis=1)
+    first = dot(aq, jnp.concatenate((ka, ka, blank), axis=0), NT, HIGH)
+    first = first - dot(ag, jnp.concatenate((inv, inv, blank), axis=0), NT, HIGH) + twice
+    mixer = first + minus
+    first_co, second_co = first[:, :K], -a1
+    rr1 = rr - ag + dot(aq, a1, NT, HIGH)
     mhi = mixer.astype(BF16).astype(F32)
     mixer = jnp.concatenate((mhi, mixer - mhi), axis=0).astype(BF16)
 
@@ -329,15 +330,21 @@
         hi, lo = split(t[:K] + t[K:])
         d2h[i] = hi
         if PD <= i < 2 * PD:
-            d2l[i - PD] = lo
-
-    for p in range(PD):
-        hi, lo = split(near_of(p, d2h) + far_of(p, lcat))
+            d2w[i] = lo
+
+    for p in range(PD):
+        hi, lo = split(near_of(p, d2h, 0) + far_of(p, lcat))
         imh[p] = hi
         iml[p] = lo
 
-    wide = [jnp.concatenate([ref[b + p] for p in range(PD)], axis=1) for ref, b in ((d2h, PD), (d2l, 0), (imh, 0), (iml, 0))]
-    pc[me] = packed_grams(jnp.concatenate(wide, axis=0))
+    def crossed(base_a, ah, al, base_b, bh, bl):
+        rows = jnp.concatenate((joined(base_a, ah), joined(base_a, al)), axis=0)
+        t = dot(rows, joined(base_b, bh)) + dot(rows, joined(base_b, bl))
+        return t[:K] + t[K:]
+
+    half = crossed(PD, d2h, d2w, 0, imh, iml) + crossed(0, imh, iml, PD, d2h, d2w)
+    half = 0.5 * half
+    pc[me] = jnp.concatenate([half[2 * i : 2 * i + 2] for i in range(8)], axis=1)
     spread_patch(pc, PC)
 
     cf[0:K, 0:K] = a1
@@ -366,13 +373,14 @@
     sign = jnp.where(is_sol, jnp.where(lane8, 1.0, 0.0), jnp.where(lane8, 0.0, -1.0))
 
     gathered_patch(pc, PC)
-    _, gg, gt, _ = unpacked_grams(jnp.sum(pc[...], axis=0))
-    a2 = eliminate(0.5 * (gg + gt), rows8)
+    total = jnp.sum(pc[...], axis=0)
+    moved = [total] + [pltpu.roll(total, 128 - K * i, 1) for i in range(1, 8)]
+    a2 = eliminate(jnp.concatenate(moved, axis=0)[:, :K], rows8)
     a2 = jnp.concatenate((a2, a2, a2, a2), axis=1)
     chi = a2.astype(BF16).astype(F32)
     coeffs = (jnp.where(row8 < 4, chi, a2 - chi) * sign).astype(BF16)
     for p in range(PD):
-        t = dot(coeffs, jnp.concatenate((d2h[PD + p], d2l[p], imh[p], iml[p]), axis=0), NN)
+        t = dot(coeffs, jnp.concatenate((d2h[PD + p], d2w[PD + p], imh[p], iml[p]), axis=0), NN)
         both_o[p] += t[:4] + t[4:]
 
     for ref, kind in ((mg, M), (pg, PA), (wg, WA), (pc, PC)):
@@ -408,7 +416,7 @@
         vm((PD, E, E), F32),
         vm((PD, E, W), F32),
         chunks, chunks, chunks, chunks,
-        three, three, three, three, three, one, one, one,
+        three, three, three, three, three, three, one, one,
         vm((PD, K, W), F32),
         vm((2 * E, PD * W), BF16),
         vm((2 * E, FL * E), BF16),
@@ -416,7 +424,8 @@
         vm((np_, 2, 128), F32),
         vm((nz, 2, 128), F32),
         vm((K, 128), F32),
-        message, message, message,
+        message, message,
+        vm((np_, 2, 128), F32),
         vm((3 * K, 128), F32),
         sem((9,)), sem((nz,)), sem((15,)), sem((15,)),
     ]

time: 42.1 us -> 42.9 us (1.019)
  Pallas kernels: 40.7 us -> 41.5 us
    pallas_call x1, Pallas kernels: 40.7 us -> 41.5 us  [on_device(): pl.pallas_call(kernel, out_shape=pltpu.VMEM((PD, 4, W), F32), in_specs=[p...]
where the time goes in v3:
time: 42.9 us; the launch traced here: 42.7 us
  Pallas kernels  41.5 us (97%)
  local copies, waits for them, and re-layouts  0.64 us (1%)
  between operations  0.64 us (1%)
    pallas_call x1, Pallas kernels, on_device(): pl.pallas_call(kernel, out_shape=pltpu.VMEM((PD, 4, W), F32), in_specs=[p...  41.5 us

profile of v3, /device:TPU:1, one launch (start us, length us, event | category | flops | bytes accessed | tf_op | source)
XLA Modules:
  0.0 42.7 jit_solution(16936396258729968123)
XLA Ops:
  0.6 41.5 %shard_map.104 = f32[8,4,384]{2,1,0:T(4,128)S(1)} custom-call(f32[8,2,384]{2,1,0:T(2,128)} %rhs_h.1, bf16[8,4,384,384]{3,2,1,0:T(8,128)(2,1)} %near_h.1, s32[4,8]{1,0:T(4,128)} %bitcast.3, f32[8,64,384]{2,1,0:T(8,128)} %up_h.1, f32[8,64,64]{2,1,0:T(8,128)} %su_h.1, s32[1,4]{1,0:T(1,128)} %fl_h.1, f32[1,4,64,64]{3,2,1,0:T(8,128)} %tr_h.1, f32[8,64,64]{2,1,0:T(8,128)} %sd_h.1, ...), custom_call_target="tpu_custom_call" | custom-call | tf_op jit(solution)/shard_map/pallas_call | solution.py:432
  42.1 0.6 %fusion = (f32[8,2,384]{2,1,0:T(2,128)}, f32[8,2,384]{2,1,0:T(2,128)}) fusion(f32[8,4,384]{2,1,0:T(4,128)S(1)} %shard_map.104), kind=kLoop, calls=%fused_computation | loop fusion | bytes 98304 | tf_op jit(solution)/shard_map/slice | solution.py:442

commit v4 on v3

--- a/solution.py
+++ b/solution.py
@@ -202,6 +202,7 @@
 
     c_fl.wait()
     src = [fl_s[0, j] for j in range(FL)]
+    spread_z(gl, ZL)
     gathered_patch(mg, M)
     low2 = lane_of((2, 128)) < E
     chosen = jnp.concatenate(
@@ -210,7 +211,6 @@
     hi, lo = split(chosen)
     lg[z] = folded(dot(hi, tst[...]) + dot(lo, tst[...]))
     spread_z(lg, L)
-    spread_z(gl, ZL)
 
     assembled(gh, sh, PD)
     c_sd.wait()
@@ -243,7 +243,7 @@
     def near_of(p, field, start):
         blocks = jnp.concatenate([near_v[p, j] for j in range(start, NB)], axis=1)
         picked = jnp.concatenate([field[ids[p][j]] for j in range(start, NB)], axis=1)
-        return dot(blocks, picked).T
+        return dot(blocks, picked).T if p % 4 != 3 else dot(picked, blocks)
 
     def far_of(p, lcat):
         far = dot(lcat, dst[p], NN)
@@ -305,12 +305,19 @@
     mhi = mixer.astype(BF16).astype(F32)
     mixer = jnp.concatenate((mhi, mixer - mhi), axis=0).astype(BF16)
 
-    gathered_patch(wg, WA)
     for kind, ref, base in (
         (OL, sl, 0), (OR, sl, 2 * PD), (WL, wh, 0), (WR, wh, 2 * PD), (WLL, wl, 0), (WRL, wl, 2 * PD)
     ):
         handle(ref.at[pl.ds(base, PD)], kind).wait_recv()
 
+    for i in range(3 * PD):
+        t = dot(mixer, jnp.concatenate((sh[i], sl[i], wh[i], wl[i]), axis=0), NN)
+        hi, lo = split(t[:K] + t[K:])
+        d2h[i] = hi
+        if PD <= i < 2 * PD:
+            d2w[i] = lo
+
+    gathered_patch(wg, WA)
     us = [wg[src[j]] for j in range(FL)]
     rs = [pltpu.roll(u, E, 1) for u in us]
     chosen = jnp.concatenate(
@@ -324,13 +331,6 @@
     local_w = folded(dot(hi, tst[...]) + dot(lo, tst[...]))
     local2 = dot(first_co, local0, NN, HIGH) + dot(second_co, local_w, NN, HIGH)
     lcat = jnp.concatenate(split(local2), axis=0)
-
-    for i in range(3 * PD):
-        t = dot(mixer, jnp.concatenate((sh[i], sl[i], wh[i], wl[i]), axis=0), NN)
-        hi, lo = split(t[:K] + t[K:])
-        d2h[i] = hi
-        if PD <= i < 2 * PD:
-            d2w[i] = lo
 
     for p in range(PD):
         hi, lo = split(near_of(p, d2h, 0) + far_of(p, lcat))

time: 42.9 us -> 41.6 us (0.970)
  Pallas kernels: 41.5 us -> 40.2 us
    pallas_call x1, Pallas kernels: 41.5 us -> 40.2 us  [on_device(): pl.pallas_call(kernel, out_shape=pltpu.VMEM((PD, 4, W), F32), in_specs=[p...]
where the time goes in v4:
time: 41.6 us; the launch traced here: 41.5 us
  Pallas kernels  40.2 us (97%)
  local copies, waits for them, and re-layouts  0.64 us (2%)
  between operations  0.64 us (2%)
    pallas_call x1, Pallas kernels, on_device(): pl.pallas_call(kernel, out_shape=pltpu.VMEM((PD, 4, W), F32), in_specs=[p...  40.2 us

profile of v4, /device:TPU:1, one launch (start us, length us, event | category | flops | bytes accessed | tf_op | source)
XLA Modules:
  0.0 41.5 jit_solution(6429327667822712455)
XLA Ops:
  0.6 40.2 %shard_map.104 = f32[8,4,384]{2,1,0:T(4,128)S(1)} custom-call(f32[8,2,384]{2,1,0:T(2,128)} %rhs_h.1, bf16[8,4,384,384]{3,2,1,0:T(8,128)(2,1)} %near_h.1, s32[4,8]{1,0:T(4,128)} %bitcast.3, f32[8,64,384]{2,1,0:T(8,128)} %up_h.1, f32[8,64,64]{2,1,0:T(8,128)} %su_h.1, s32[1,4]{1,0:T(1,128)} %fl_h.1, f32[1,4,64,64]{3,2,1,0:T(8,128)} %tr_h.1, f32[8,64,64]{2,1,0:T(8,128)} %sd_h.1, ...), custom_call_target="tpu_custom_call" | custom-call | tf_op jit(solution)/shard_map/pallas_call | solution.py:432
  40.8 0.6 %fusion = (f32[8,2,384]{2,1,0:T(2,128)}, f32[8,2,384]{2,1,0:T(2,128)}) fusion(f32[8,4,384]{2,1,0:T(4,128)S(1)} %shard_map.104), kind=kLoop, calls=%fused_computation | loop fusion | bytes 98304 | tf_op jit(solution)/shard_map/slice | solution.py:442

commit v5 on v4

--- a/solution.py
+++ b/solution.py
@@ -34,7 +34,7 @@
 def eliminate(top, *others):
     a = jnp.concatenate((top, *others), axis=0)
     lanes = lane_of(a.shape)
-    group = 4
+    group = 8
     for base in range(0, K, group):
         columns = [jnp.broadcast_to(a[:, k : k + 1], a.shape) for k in range(base, base + group)]
         for i in range(group):
@@ -305,17 +305,23 @@
     mhi = mixer.astype(BF16).astype(F32)
     mixer = jnp.concatenate((mhi, mixer - mhi), axis=0).astype(BF16)
 
-    for kind, ref, base in (
-        (OL, sl, 0), (OR, sl, 2 * PD), (WL, wh, 0), (WR, wh, 2 * PD), (WLL, wl, 0), (WRL, wl, 2 * PD)
-    ):
-        handle(ref.at[pl.ds(base, PD)], kind).wait_recv()
-
-    for i in range(3 * PD):
+    def mixed(i):
         t = dot(mixer, jnp.concatenate((sh[i], sl[i], wh[i], wl[i]), axis=0), NN)
         hi, lo = split(t[:K] + t[K:])
         d2h[i] = hi
         if PD <= i < 2 * PD:
             d2w[i] = lo
+
+    for i in range(PD, 2 * PD):
+        mixed(i)
+    for p in range(PD):
+        nf[p] = dot(near_v[p, 0], d2h[PD + p]).T
+
+    for base, kinds in ((0, (OL, WL, WLL)), (2 * PD, (OR, WR, WRL))):
+        for kind, ref in zip(kinds, (sl, wh, wl)):
+            handle(ref.at[pl.ds(base, PD)], kind).wait_recv()
+        for i in range(base, base + PD):
+            mixed(i)
 
     gathered_patch(wg, WA)
     us = [wg[src[j]] for j in range(FL)]
@@ -333,7 +339,7 @@
     lcat = jnp.concatenate(split(local2), axis=0)
 
     for p in range(PD):
-        hi, lo = split(near_of(p, d2h, 0) + far_of(p, lcat))
+        hi, lo = split(nf[p] + near_of(p, d2h, 1) + far_of(p, lcat))
         imh[p] = hi
         iml[p] = lo
 

time: 41.6 us -> 41 us (0.986)
  Pallas kernels: 40.2 us -> 39.6 us
    pallas_call x1, Pallas kernels: 40.2 us -> 39.6 us  [on_device(): pl.pallas_call(kernel, out_shape=pltpu.VMEM((PD, 4, W), F32), in_specs=[p...]
where the time goes in v5:
time: 41 us; the launch traced here: 40.8 us
  Pallas kernels  39.6 us (97%)
  local copies, waits for them, and re-layouts  0.64 us (2%)
  between operations  0.64 us (2%)
    pallas_call x1, Pallas kernels, on_device(): pl.pallas_call(kernel, out_shape=pltpu.VMEM((PD, 4, W), F32), in_specs=[p...  39.6 us

profile of v5, /device:TPU:1, one launch (start us, length us, event | category | flops | bytes accessed | tf_op | source)
XLA Modules:
  0.0 40.8 jit_solution(16249564603312401777)
XLA Ops:
  0.6 39.6 %shard_map.104 = f32[8,4,384]{2,1,0:T(4,128)S(1)} custom-call(f32[8,2,384]{2,1,0:T(2,128)} %rhs_h.1, bf16[8,4,384,384]{3,2,1,0:T(8,128)(2,1)} %near_h.1, s32[4,8]{1,0:T(4,128)} %bitcast.3, f32[8,64,384]{2,1,0:T(8,128)} %up_h.1, f32[8,64,64]{2,1,0:T(8,128)} %su_h.1, s32[1,4]{1,0:T(1,128)} %fl_h.1, f32[1,4,64,64]{3,2,1,0:T(8,128)} %tr_h.1, f32[8,64,64]{2,1,0:T(8,128)} %sd_h.1, ...), custom_call_target="tpu_custom_call" | custom-call | tf_op jit(solution)/shard_map/pallas_call | solution.py:438
  40.2 0.6 %fusion = (f32[8,2,384]{2,1,0:T(2,128)}, f32[8,2,384]{2,1,0:T(2,128)}) fusion(f32[8,4,384]{2,1,0:T(4,128)S(1)} %shard_map.104), kind=kLoop, calls=%fused_computation | loop fusion | bytes 98304 | tf_op jit(solution)/shard_map/slice | solution.py:448
